TPU v7x, 256 devices: a whole 4x4x8 slice. The times are simulated.
256 devices in a mesh: row: 8 (over x, z_lo), col: 8 (over z_hi, core), depth: 4 (over y).
Axes of the slice: x: 4, y: 4, z: 8 (z_hi: 4, z_lo: 2; z = z_hi * 2 + z_lo), core: 2. Of those that a mesh axis runs over, the one named last changes fastest.
Arguments:
- alignment_matrix: bfloat16 [128, 768, 256], P('depth', 'col'), may hold values from -6 to 6
- twin_linear_matrix: bfloat16 [256, 64], replicated, may hold values from -0.375 to 0.375
- final_matrix: bfloat16 [1024, 128], replicated, may hold values from -2 to 2
- final_offset: float32 [128], replicated, may hold values from -3 to 3
- adjoint_incoming: bfloat16 [768, 768, 128], P('row', ('col', 'depth')), may hold values from -6 to 6
Outputs:
- contact_delta: bfloat16 [768, 768, 128], P('row', ('col', 'depth'))
- alignment_adjoint: float32 [128, 768, 256], P('depth', 'col')
- grad_w_out: float32 [1024, 128], replicated
- grad_b_out: float32 [128], replicated
All inputs are finite; a program needn't handle non-finite values.
Results may differ from a plain program's by a relative error of at most 0.007.
Values may be sent and summed in bfloat16 or wider, within the bound.
No kernel may reach another device: no remote copies, remote signals or barrier semaphores. Data moves between devices by JAX's collectives and lax.ppermute only.
A program may use at most 128 MiB of HBM per device.

v0:
```python
import jax
import jax.numpy as jnp
from jax import lax
from jax.sharding import PartitionSpec as P

epsilon = 1e-05


def in_one(arrays, axis):
    vector, at, gathered = (jnp.concatenate([a.reshape(-1) for a in arrays]), 0, [])
    running = lax.psum(vector, axis)
    for a in arrays:
        gathered.append(running[at : at + a.size].reshape(a.shape))
        at += a.size
    return tuple(gathered)


def broadcast(shard, axis, root):
    return lax.dynamic_index_in_dim(lax.all_gather(shard, axis), root, 0, keepdims=False)


def copy_for_each(shard, axis):
    copies = jnp.broadcast_to(shard, (lax.axis_size(axis), *shard.shape))
    return lax.all_to_all(copies, axis, split_axis=0, concat_axis=0, tiled=True)


def of_everyone(shard, axis):
    everything = copy_for_each(shard, axis)
    return jnp.sum(everything, axis=0)


def standardize_channels(values):
    centre = jnp.mean(values, axis=-1, keepdims=True)
    spread = jnp.mean(jnp.square(values - centre), axis=-1, keepdims=True)
    return (values - centre) * lax.rsqrt(spread + epsilon)


def body(alignment_matrix, twin_linear_matrix, final_matrix, final_offset, adjoint_incoming):
    alignment_share, amino_share, discarded_item = alignment_matrix.shape
    latent_features = twin_linear_matrix.shape[1] // 2
    row_count = lax.axis_size("row")
    col_count = lax.axis_size("col")
    depth_count = lax.axis_size("depth")
    crop_length = amino_share * col_count
    block_i = crop_length // row_count
    quarter = amino_share // depth_count
    row_idx = lax.axis_index("row")
    col_idx = lax.axis_index("col")
    standardized_alignment, standardize_backprop = jax.vjp(
        standardize_channels, alignment_matrix.astype(jnp.float32)
    )
    normed = standardized_alignment.astype(jnp.bfloat16)
    panels = jnp.dot(normed, twin_linear_matrix, preferred_element_type=jnp.float32).astype(
        jnp.bfloat16
    )
    left_local = panels[..., :latent_features]
    right_local = panels[..., latent_features:]
    left_every = lax.all_gather(left_local, "col", axis=1, tiled=True)
    left_rows = lax.dynamic_slice_in_dim(left_every, row_idx * block_i, block_i, 1)
    left_seqs = lax.all_gather(left_rows, "depth", axis=0, tiled=True)
    right_seqs = lax.all_to_all(right_local, "depth", split_axis=1, concat_axis=0, tiled=True)
    seq_count = left_seqs.shape[0]
    summed = jnp.einsum(
        "sje,sic->jice", right_seqs, left_seqs, preferred_element_type=jnp.float32
    ).reshape(quarter, block_i, latent_features * latent_features)
    outer_mean = (summed / seq_count).astype(jnp.bfloat16)
    pair_cols = jnp.dot(outer_mean, final_matrix, preferred_element_type=jnp.float32) + final_offset
    contact_delta = jnp.transpose(pair_cols, (1, 0, 2)).astype(jnp.bfloat16)
    adjoint_kronecker = (
        jnp.einsum(
            "gtz,vz->gtv", adjoint_incoming, final_matrix, preferred_element_type=jnp.float32
        )
        / seq_count
    ).astype(jnp.bfloat16)
    grad_four = adjoint_kronecker.reshape(block_i, quarter, latent_features, latent_features)
    adjoint_leftside = jnp.einsum(
        "ijce,sje->sic", grad_four, right_seqs, preferred_element_type=jnp.float32
    )
    grad_right = jnp.einsum(
        "ijce,sic->sje", grad_four, left_seqs, preferred_element_type=jnp.float32
    )
    w_local = jnp.einsum(
        "jif,ijo->fo", outer_mean, adjoint_incoming, preferred_element_type=jnp.float32
    )
    b_local = jnp.sum(adjoint_incoming.astype(jnp.float32), axis=(0, 1))
    weight_gradient, bias_gradient = in_one((w_local, b_local), ("row", "col", "depth"))
    left_back, right_back = (
        lax.all_to_all(adjoint_leftside, "depth", split_axis=0, concat_axis=1, tiled=True),
        lax.all_to_all(grad_right, "depth", split_axis=0, concat_axis=1, tiled=True),
    )
    left_back = jnp.sum(
        left_back.reshape(alignment_share, depth_count, block_i, latent_features), axis=1
    )
    left_summed = lax.psum(left_back, "col")
    owner_row = col_idx * amino_share // block_i
    left_full = broadcast(left_summed.astype(jnp.bfloat16), "row", owner_row).astype(
        left_summed.dtype
    )
    right_full = of_everyone(right_back, "row")
    both_grads = jnp.concatenate([left_full, right_full], axis=-1)
    grad_panels = both_grads.astype(jnp.bfloat16)
    standardized_adjoint = jnp.einsum(
        "slk,mk->slm", grad_panels, twin_linear_matrix, preferred_element_type=jnp.float32
    )
    alignment_adjoint = standardize_backprop(standardized_adjoint)[0]
    return (
        contact_delta,
        alignment_adjoint,
        weight_gradient / crop_length,
        bias_gradient / crop_length,
    )


def solution(mesh):
    in_specs = (P("depth", "col", None), P(), P(), P(), P("row", ("col", "depth"), None))
    out_specs = (P("row", ("col", "depth"), None), P("depth", "col", None), P(), P())
    return jax.shard_map(body, mesh=mesh, in_specs=in_specs, out_specs=out_specs, check_vma=False)
```

profile of v0, /device:TPU:1, one launch (start us, length us, event | category | flops | bytes accessed | tf_op | source)
XLA Modules:
  0.0 472.1 jit_solution(5661845479301086679)
XLA Ops:
  18.8 5.0 %all-to-all-start = ((bf16[4,2,12288]{2,1,0:T(2,128)(2,1)}), bf16[4,2,12288]{2,1,0:T(2,128)(2,1)S(1)}, u32[]{:S(2)}, u32[]{:S(2)}) async-start(bf16[4,2,12288]{2,1,0:T(2,128)(2,1)} %reshape.73), calls=%async_computation | async-start | bytes 393216 | tf_op jit(solution)/shard_map/all_to_all | solution.py:61
  23.8 3.5 multiply_convert_fusion.1
  27.3 8.5 %copy.39 = bf16[96,24,1024]{0,2,1:T(8,128)(2,1)} copy(bf16[96,24,1024]{2,1,0:T(8,128)(2,1)} %multiply_convert_fusion.1) | data formatting | bytes 9437184 | tf_op jit(solution)/shard_map/convert_element_type | solution.py:74
  37.9 5.1 %convolution_bitcast_fusion.1 = f32[128,96,32]{0,1,2:T(8,128)S(1)} fusion(bf16[96,24,32,32]{0,3,2,1:T(8,128)(2,1)} %bitcast.63, bf16[128,24,32,1]{0,2,1,3:T(8,128)(2,1)} %reshape.66), kind=kOutput, calls=%fused_computation.20 | convolution fusion | flops 603979776 | bytes 6488064 | tf_op jit(solution)/shard_map/ijce,sje->sic/dot_general | solution.py:76
  44.9 4.8 %all-to-all-start.1 = ((f32[128,96,32]{1,2,0:T(8,128)}), f32[128,96,32]{1,2,0:T(8,128)}, u32[]{:S(2)}, u32[]{:S(2)}) async-start(f32[128,96,32]{1,2,0:T(8,128)} %copy.41), calls=%async_computation.1 | async-start | bytes 4194304 | tf_op jit(solution)/shard_map/all_to_all | solution.py:88
  50.0 24.5 %all-to-all-done.1 = f32[128,96,32]{1,2,0:T(8,128)} async-done(((f32[128,96,32]{1,2,0:T(8,128)}), f32[128,96,32]{1,2,0:T(8,128)}, u32[]{:S(2)}, u32[]{:S(2)}) %all-to-all-start.1) | async-done | bytes 1572896 | tf_op jit(solution)/shard_map/all_to_all | solution.py:88
  74.6 2.7 reduce_sum.82
  77.3 13.4 %all-gather.4.cloned.1.call-done = bf16[32,768,32]{2,0,1:T(8,128)(2,1)} async-done(((bf16[32,96,32]{2,0,1:T(8,128)(2,1)}), bf16[32,768,32]{2,0,1:T(8,128)(2,1)}) %all-gather.4.cloned.1.call-update) | async-done | bytes 1572880 | tf_op jit(solution)/shard_map/all_gather | solution.py:58
  92.6 13.8 %all_gather.13 = bf16[128,96,32]{1,2,0:T(8,128)(2,1)S(1)} all-gather(bf16[32,96,32]{1,2,0:T(8,128)(2,1)S(1)} %copy.32), channel_id=1, replica_groups=mesh['row'=8,'col'=8,'depth'=4] {'depth'}, dimensions={0}, use_global_device_ids=true | all-gather | bytes 983040 | tf_op jit(solution)/shard_map/all_gather | solution.py:60
  106.4 5.0 %convolution_bitcast_fusion.2 = f32[128,24,32]{0,2,1:T(8,128)S(1)} fusion(bf16[96,24,32,32]{0,3,2,1:T(8,128)(2,1)} %bitcast.64, bf16[128,96,32]{1,2,0:T(8,128)(2,1)S(1)} %all_gather.13), kind=kOutput, calls=%fused_computation.25 | convolution fusion | flops 603979776 | bytes 5898240 | tf_op jit(solution)/shard_map/ijce,sic->sje/dot_general | solution.py:79
  115.5 2.8 reshape.75
  118.3 3.5 all-to-all-start.2
  121.8 9.1 %fusion = bf16[24,96,32,32]{3,2,0,1:T(8,128)(2,1)} fusion(bf16[128,96,32,1]{0,2,3,1:T(8,128)(2,1)S(1)} %copy.48, bf16[128,24,32,1]{0,2,1,3:T(8,128)(2,1)S(1)} %copy-done.7), kind=kOutput, calls=%fused_computation.1 | convolution fusion | flops 608698368 | bytes 5701632 | tf_op jit(solution)/shard_map/sje,sic->jice/dot_general | solution.py:63
  130.9 20.1 %copy.37 = bf16[24,96,32,32]{1,3,2,0:T(8,128)(2,1)} copy(bf16[24,96,32,32]{3,2,0,1:T(8,128)(2,1)} %fusion) | data formatting | bytes 9437184 | tf_op jit(solution)/shard_map/convert_element_type | solution.py:66
  151.5 2.5 reduce.2
  159.8 2.5 broadcast_in_dim.4
  162.3 4.7 all-to-all-start.3
  167.3 4.3 convolution_bitcast_fusion
  172.6 66.0 %all-reduce.4 = bf16[32,96,32]{1,2,0:T(8,128)(2,1)} all-reduce(f32[32,96,32]{1,2,0:T(8,128)S(1)} %copy-done.6), channel_id=1, replica_groups=mesh['row'=8,'col'=8,'depth'=4] {'col'}, use_global_device_ids=true, to_apply=%region_3.0 | all-reduce | flops 98304 | bytes 589824 | tf_op jit(solution)/shard_map/psum | solution.py:94
  238.7 4.6 fusion.19
  244.3 205.4 %all-reduce.3.cloned.1.call-done = f32[131200]{0:T(1024)} async-done(((f32[131200]{0:T(1024)}), f32[131200]{0:T(1024)}) %all-reduce.3.cloned.1.call-update) | async-done | bytes 524816 | tf_op jit(solution)/shard_map/psum | solution.py:11
  453.8 2.8 reduce_sum.83
  456.6 3.2 multiply_reduce_fusion
  461.5 3.2 fusion.7
  (60 shorter events, 35.2 us)
Async XLA Ops:
  8.0 15.8 %copy-start = (bf16[1024,128]{1,0:T(8,128)(2,1)S(1)}, bf16[1024,128]{1,0:T(8,128)(2,1)}, u32[]{:S(2)}) copy-start(bf16[1024,128]{1,0:T(8,128)(2,1)} %param.7) | copy-start | bytes 786436
  8.0 4.7 copy-start.1
  8.0 4.7 copy-start.8
  8.0 82.6 %all-gather.4.cloned.1.call-start = ((), (), s32[]{:S(2)}) async-start(), calls=%async_computation.4 | async-start | bytes 7077888 | tf_op jit(solution)/shard_map/all_gather | solution.py:58
  14.1 9.8 %copy-start.3 = (bf16[96,24,128]{2,1,0:T(8,128)(2,1)S(1)}, bf16[96,24,128]{2,1,0:T(8,128)(2,1)}, u32[]{:S(2)}) copy-start(bf16[96,24,128]{2,1,0:T(8,128)(2,1)} %param.9) | copy-start | bytes 1769476
  18.8 17.0 %all-to-all-start = ((bf16[4,2,12288]{2,1,0:T(2,128)(2,1)}), bf16[4,2,12288]{2,1,0:T(2,128)(2,1)S(1)}, u32[]{:S(2)}, u32[]{:S(2)}) async-start(bf16[4,2,12288]{2,1,0:T(2,128)(2,1)} %reshape.73), calls=%async_computation | async-start | bytes 393216 | tf_op jit(solution)/shard_map/all_to_all | solution.py:61
  44.9 4.8 %copy-start.4 = (bf16[96,24,128]{2,1,0:T(8,128)(2,1)S(1)}, bf16[96,24,128]{2,1,0:T(8,128)(2,1)}, u32[]{:S(2)}) copy-start(bf16[96,24,128]{2,1,0:T(8,128)(2,1)} %param.9) | copy-start | bytes 1769476
  44.9 29.7 %all-to-all-start.1 = ((f32[128,96,32]{1,2,0:T(8,128)}), f32[128,96,32]{1,2,0:T(8,128)}, u32[]{:S(2)}, u32[]{:S(2)}) async-start(f32[128,96,32]{1,2,0:T(8,128)} %copy.41), calls=%async_computation.1 | async-start | bytes 4194304 | tf_op jit(solution)/shard_map/all_to_all | solution.py:88
  106.4 5.0 %copy-start.2 = (bf16[128,96,32]{1,2,0:T(8,128)(2,1)}, bf16[128,96,32]{1,2,0:T(8,128)(2,1)S(1)}, u32[]{:S(2)}) copy-start(bf16[128,96,32]{1,2,0:T(8,128)(2,1)S(1)} %all_gather.13) | copy-start | bytes 2359300
  111.4 10.4 %copy-start.7 = (bf16[128,24,32,1]{0,2,1,3:T(8,128)(2,1)S(1)}, bf16[128,24,32,1]{0,2,1,3:T(8,128)(2,1)}, u32[]{:S(2)}) copy-start(bf16[128,24,32,1]{0,2,1,3:T(8,128)(2,1)} %reshape.66) | copy-start | bytes 589828
  118.3 32.7 %all-to-all-start.2 = ((f32[4,1,24576]{2,1,0:T(1,128)}), f32[4,1,24576]{2,1,0:T(1,128)S(1)}, u32[]{:S(2)}, u32[]{:S(2)}) async-start(f32[4,1,24576]{2,1,0:T(1,128)} %reshape.75), calls=%async_computation.2 | async-start | bytes 786432 | tf_op jit(solution)/shard_map/all_to_all | solution.py:89
  162.3 5.0 %copy-start.5 = (bf16[96,24,128]{2,1,0:T(8,128)(2,1)S(1)}, bf16[96,24,128]{2,1,0:T(8,128)(2,1)}, u32[]{:S(2)}) copy-start(bf16[96,24,128]{2,1,0:T(8,128)(2,1)} %param.9) | copy-start | bytes 1769476
  162.3 291.5 %all-to-all-start.3 = ((f32[8,32,96,32]{2,3,1,0:T(8,128)}), f32[8,32,96,32]{2,3,1,0:T(8,128)}, u32[]{:S(2)}, u32[]{:S(2)}) async-start(f32[8,32,96,32]{2,3,1,0:T(8,128)} %broadcast_in_dim.4), calls=%async_computation.3 | async-start | bytes 8388608 | tf_op jit(solution)/shard_map/all_to_all | solution.py:24
  167.0 282.8 %all-reduce.3.cloned.1.call-start = ((), (), s32[]{:S(2)}) async-start(), calls=%async_computation.5 | async-start | bytes 1056768 | tf_op jit(solution)/shard_map/psum | solution.py:11
  167.3 5.3 %copy-start.6 = (f32[32,96,32]{1,2,0:T(8,128)S(1)}, f32[32,96,32]{1,2,0:T(8,128)}, u32[]{:S(2)}) copy-start(f32[32,96,32]{1,2,0:T(8,128)} %reduce_sum.82) | copy-start | bytes 1179652
  167.3 71.4 %copy-start.9 = (f32[128]{0:T(128)S(1)}, f32[128]{0:T(128)}, u32[]{:S(2)}) copy-start(f32[128]{0:T(128)} %param.8) | copy-start | bytes 1540
  172.5 280.3 %all-gather.6.cloned.1.call-start = ((), (), s32[]{:S(2)}) async-start(), calls=%async_computation.6 | async-start | bytes 2359296 | tf_op jit(solution)/shard_map/all_gather | solution.py:19
Sparse Core Ops, SparseCore 0:
  16.3 74.2 all-gather.3
  173.9 275.8 all-reduce.2
Sparse Core Ops, SparseCore 1:
  238.7 60.2 all-gather.5
where the time goes:
time: 474 us; the launch traced here: 472 us
  waiting for transfers between devices  243 us (51%)
  blocking collectives  79.8 us (17%)
  local copies, waits for them, and re-layouts  57 us (12%)
  matrix products  36.2 us (8%)
  other arithmetic  21.6 us (5%)
  starting transfers between devices  18.3 us (4%)
  between operations  15.8 us (3%)
    psum x1, waiting for transfers between devices, in_one(): running = lax.psum(vector, axis)  205 us
    psum x1, blocking collectives, body(): left_summed = lax.psum(left_back, 'col')  66 us
    all_to_all x1, waiting for transfers between devices, body(): lax.all_to_all(adjoint_leftside, 'depth', split_axis=0, concat_axis=1, ti...  24.5 us
    convert_element_type x1, local copies, waits for them, and re-layouts, body(): outer_mean = (summed / seq_count).astype(jnp.bfloat16)  20.1 us
    all_gather x1, blocking collectives, body(): left_seqs = lax.all_gather(left_rows, 'depth', axis=0, tiled=True)  13.8 us
    all_gather x1, waiting for transfers between devices, body(): left_every = lax.all_gather(left_local, 'col', axis=1, tiled=True)  13.4 us
  transfers between devices with their start and end apart: 7, of which 3 were waited for; matrix products, arithmetic and copies ran while one was open for 15% of the time, Pallas kernels for 0%

commit v1 on v0

--- a/solution.py
+++ b/solution.py
@@ -85,7 +85,15 @@
     b_local = jnp.sum(adjoint_incoming.astype(jnp.float32), axis=(0, 1))
     weight_gradient, bias_gradient = in_one((w_local, b_local), ("row", "col", "depth"))
     left_back, right_back = (
-        lax.all_to_all(adjoint_leftside, "depth", split_axis=0, concat_axis=1, tiled=True),
+        jnp.concatenate(
+            lax.all_to_all(
+                jnp.stack(jnp.split(adjoint_leftside, lax.axis_size("depth"), axis=0)),
+                "depth",
+                0,
+                0,
+            ),
+            axis=1,
+        ),
         lax.all_to_all(grad_right, "depth", split_axis=0, concat_axis=1, tiled=True),
     )
     left_back = jnp.sum(

time: 474 us -> 481 us (1.015)
  waiting for transfers between devices: 243 us -> 231 us
  local copies, waits for them, and re-layouts: 57 us -> 68.2 us
    all_gather x1, waiting for transfers between devices: 13.4 us -> 0.01 us  [body(): left_every = lax.all_gather(left_local, 'col', axis=1, tiled=True)]
    another operation x0 -> x5, local copies, waits for them, and re-layouts: none -> 13.1 us  [body(): jnp.stack(jnp.split(adjoint_leftside, lax.axis_size('depth'), axis=0))]
  transfers between devices with their start and end apart: 7 -> 7, of which waited for: 3 -> 2; matrix products, arithmetic and copies ran while one was open for 15% -> 18% of each run, Pallas kernels for 0% -> 0%
where the time goes in v1:
time: 481 us; the launch traced here: 479 us
  waiting for transfers between devices  231 us (48%)
  blocking collectives  83.5 us (17%)
  local copies, waits for them, and re-layouts  68.2 us (14%)
  matrix products  36.1 us (8%)
  other arithmetic  24.7 us (5%)
  starting transfers between devices  19.1 us (4%)
  between operations  15.9 us (3%)
    psum x1, waiting for transfers between devices, in_one(): running = lax.psum(vector, axis)  207 us
    psum x1, blocking collectives, body(): left_summed = lax.psum(left_back, 'col')  70.2 us
    all_to_all x1, waiting for transfers between devices, body(): lax.all_to_all(jnp.stack(jnp.split(adjoint_leftside, lax.axis_size('depth...  24.4 us
    convert_element_type x1, local copies, waits for them, and re-layouts, body(): outer_mean = (summed / seq_count).astype(jnp.bfloat16)  20.1 us
    all_gather x1, blocking collectives, body(): left_seqs = lax.all_gather(left_rows, 'depth', axis=0, tiled=True)  13.2 us
    another operation x5, local copies, waits for them, and re-layouts, body(): jnp.stack(jnp.split(adjoint_leftside, lax.axis_size('depth'), axis=0))  13.1 us
  transfers between devices with their start and end apart: 7, of which 2 were waited for; matrix products, arithmetic and copies ran while one was open for 18% of the time, Pallas kernels for 0%

profile of v1, /device:TPU:1, one launch (start us, length us, event | category | flops | bytes accessed | tf_op | source)
XLA Modules:
  0.0 478.8 jit_solution(18174001018659778824)
XLA Ops:
  18.8 5.0 %all-to-all-start = ((bf16[4,2,12288]{2,1,0:T(2,128)(2,1)}), bf16[4,2,12288]{2,1,0:T(2,128)(2,1)S(1)}, u32[]{:S(2)}, u32[]{:S(2)}) async-start(bf16[4,2,12288]{2,1,0:T(2,128)(2,1)} %reshape.72), calls=%async_computation | async-start | bytes 393216 | tf_op jit(solution)/shard_map/all_to_all | solution.py:61
  23.8 3.5 multiply_convert_fusion.1
  27.4 8.5 %copy.60 = bf16[96,24,1024]{0,2,1:T(8,128)(2,1)} copy(bf16[96,24,1024]{2,1,0:T(8,128)(2,1)} %multiply_convert_fusion.1) | data formatting | bytes 9437184 | tf_op jit(solution)/shard_map/convert_element_type | solution.py:74
  37.9 5.0 %convolution_bitcast_fusion.1 = f32[128,96,32]{0,1,2:T(8,128)S(1)} fusion(bf16[96,24,32,32]{0,3,2,1:T(8,128)(2,1)} %bitcast.70, bf16[128,24,32,1]{0,2,1,3:T(8,128)(2,1)S(1)} %reshape.65), kind=kOutput, calls=%fused_computation.25 | convolution fusion | flops 603979776 | bytes 6488064 | tf_op jit(solution)/shard_map/ijce,sje->sic/dot_general | solution.py:76
  42.9 3.5 slice_bitcast_fusion.3
  46.5 2.7 copy.65
  51.9 2.7 copy.63
  56.0 3.1 pad_maximum_fusion
  59.1 4.6 all-to-all-start.1
  64.0 24.4 %all-to-all-done.1 = f32[4,32,96,32]{2,3,1,0:T(8,128)} async-done(((f32[4,32,96,32]{2,3,1,0:T(8,128)}), f32[4,32,96,32]{2,3,1,0:T(8,128)}, u32[]{:S(2)}, u32[]{:S(2)}) %all-to-all-start.1) | async-done | bytes 1572896 | tf_op jit(solution)/shard_map/all_to_all | solution.py:89
  93.1 13.2 %all_gather.13 = bf16[128,96,32]{1,2,0:T(8,128)(2,1)S(1)} all-gather(bf16[32,96,32]{1,2,0:T(8,128)(2,1)S(1)} %copy.53), channel_id=1, replica_groups=mesh['row'=8,'col'=8,'depth'=4] {'depth'}, dimensions={0}, use_global_device_ids=true | all-gather | bytes 983040 | tf_op jit(solution)/shard_map/all_gather | solution.py:60
  106.4 5.0 %convolution_bitcast_fusion.2 = f32[128,24,32]{0,2,1:T(8,128)S(1)} fusion(bf16[96,24,32,32]{0,3,2,1:T(8,128)(2,1)} %bitcast.71, bf16[128,96,32]{1,2,0:T(8,128)(2,1)S(1)} %all_gather.13), kind=kOutput, calls=%fused_computation.30 | convolution fusion | flops 603979776 | bytes 5898240 | tf_op jit(solution)/shard_map/ijce,sic->sje/dot_general | solution.py:79
  115.4 2.8 reshape.74
  118.2 3.5 all-to-all-start.2
  121.7 9.1 %fusion = bf16[24,96,32,32]{3,2,0,1:T(8,128)(2,1)} fusion(bf16[128,96,32,1]{0,2,3,1:T(8,128)(2,1)S(1)} %copy.74, bf16[128,24,32,1]{0,2,1,3:T(8,128)(2,1)S(1)} %copy-done.8), kind=kOutput, calls=%fused_computation.1 | convolution fusion | flops 608698368 | bytes 5701632 | tf_op jit(solution)/shard_map/sje,sic->jice/dot_general | solution.py:63
  130.8 20.1 %copy.58 = bf16[24,96,32,32]{1,3,2,0:T(8,128)(2,1)} copy(bf16[24,96,32,32]{3,2,0,1:T(8,128)(2,1)} %fusion) | data formatting | bytes 9437184 | tf_op jit(solution)/shard_map/convert_element_type | solution.py:66
  162.2 5.9 %all-to-all-start.3 = ((f32[8,32,96,32]{2,3,1,0:T(8,128)}), f32[8,32,96,32]{2,3,1,0:T(8,128)}, u32[]{:S(2)}, u32[]{:S(2)}) async-start(f32[8,32,96,32]{2,3,1,0:T(8,128)} %broadcast_in_dim.4), calls=%async_computation.3 | async-start | bytes 8388608 | tf_op jit(solution)/shard_map/all_to_all | solution.py:24
  168.2 4.3 convolution_bitcast_fusion
  173.5 70.2 %all-reduce.4 = bf16[32,96,32]{1,2,0:T(8,128)(2,1)} all-reduce(f32[32,96,32]{1,2,0:T(8,128)S(1)} %copy-done.6), channel_id=1, replica_groups=mesh['row'=8,'col'=8,'depth'=4] {'col'}, use_global_device_ids=true, to_apply=%region_3.0 | all-reduce | flops 98304 | bytes 589824 | tf_op jit(solution)/shard_map/psum | solution.py:102
  243.7 4.6 fusion.19
  249.4 207.0 %all-reduce.3.cloned.1.call-done = f32[131200]{0:T(1024)} async-done(((f32[131200]{0:T(1024)}), f32[131200]{0:T(1024)}) %all-reduce.3.cloned.1.call-update) | async-done | bytes 524816 | tf_op jit(solution)/shard_map/psum | solution.py:11
  460.5 2.8 reduce_sum.83
  463.3 3.2 multiply_reduce_fusion
  468.2 3.2 fusion.7
  (67 shorter events, 44.8 us)
Async XLA Ops:
  8.0 15.8 %copy-start = (bf16[1024,128]{1,0:T(8,128)(2,1)S(1)}, bf16[1024,128]{1,0:T(8,128)(2,1)}, u32[]{:S(2)}) copy-start(bf16[1024,128]{1,0:T(8,128)(2,1)} %param.7) | copy-start | bytes 786436
  8.0 4.7 copy-start.1
  8.0 4.7 copy-start.9
  8.0 83.1 %all-gather.4.cloned.1.call-start = ((), (), s32[]{:S(2)}) async-start(), calls=%async_computation.4 | async-start | bytes 7077888 | tf_op jit(solution)/shard_map/all_gather | solution.py:58
  14.1 9.8 %copy-start.3 = (bf16[96,24,128]{2,1,0:T(8,128)(2,1)S(1)}, bf16[96,24,128]{2,1,0:T(8,128)(2,1)}, u32[]{:S(2)}) copy-start(bf16[96,24,128]{2,1,0:T(8,128)(2,1)} %param.9) | copy-start | bytes 1769476
  18.8 17.0 %all-to-all-start = ((bf16[4,2,12288]{2,1,0:T(2,128)(2,1)}), bf16[4,2,12288]{2,1,0:T(2,128)(2,1)S(1)}, u32[]{:S(2)}, u32[]{:S(2)}) async-start(bf16[4,2,12288]{2,1,0:T(2,128)(2,1)} %reshape.72), calls=%async_computation | async-start | bytes 393216 | tf_op jit(solution)/shard_map/all_to_all | solution.py:61
  37.2 0.7 copy-start.7
  59.1 4.6 copy-start.4
  59.1 29.3 %all-to-all-start.1 = ((f32[4,32,96,32]{2,3,1,0:T(8,128)}), f32[4,32,96,32]{2,3,1,0:T(8,128)}, u32[]{:S(2)}, u32[]{:S(2)}) async-start(f32[4,32,96,32]{2,3,1,0:T(8,128)} %pad_maximum_fusion), calls=%async_computation.1 | async-start | bytes 4194304 | tf_op jit(solution)/shard_map/all_to_all | solution.py:89
  106.4 5.0 %copy-start.2 = (bf16[128,96,32]{1,2,0:T(8,128)(2,1)}, bf16[128,96,32]{1,2,0:T(8,128)(2,1)S(1)}, u32[]{:S(2)}) copy-start(bf16[128,96,32]{1,2,0:T(8,128)(2,1)S(1)} %all_gather.13) | copy-start | bytes 2359300
  111.3 10.4 %copy-start.8 = (bf16[128,24,32,1]{0,2,1,3:T(8,128)(2,1)S(1)}, bf16[128,24,32,1]{0,2,1,3:T(8,128)(2,1)}, u32[]{:S(2)}) copy-start(bf16[128,24,32,1]{0,2,1,3:T(8,128)(2,1)} %copy-done.7) | copy-start | bytes 589828
  118.2 32.7 %all-to-all-start.2 = ((f32[4,1,24576]{2,1,0:T(1,128)}), f32[4,1,24576]{2,1,0:T(1,128)S(1)}, u32[]{:S(2)}, u32[]{:S(2)}) async-start(f32[4,1,24576]{2,1,0:T(1,128)} %reshape.74), calls=%async_computation.2 | async-start | bytes 786432 | tf_op jit(solution)/shard_map/all_to_all | solution.py:97
  162.2 5.9 %copy-start.5 = (bf16[96,24,128]{2,1,0:T(8,128)(2,1)S(1)}, bf16[96,24,128]{2,1,0:T(8,128)(2,1)}, u32[]{:S(2)}) copy-start(bf16[96,24,128]{2,1,0:T(8,128)(2,1)} %param.9) | copy-start | bytes 1769476
  162.2 298.3 %all-to-all-start.3 = ((f32[8,32,96,32]{2,3,1,0:T(8,128)}), f32[8,32,96,32]{2,3,1,0:T(8,128)}, u32[]{:S(2)}, u32[]{:S(2)}) async-start(f32[8,32,96,32]{2,3,1,0:T(8,128)} %broadcast_in_dim.4), calls=%async_computation.3 | async-start | bytes 8388608 | tf_op jit(solution)/shard_map/all_to_all | solution.py:24
  168.1 288.3 %all-reduce.3.cloned.1.call-start = ((), (), s32[]{:S(2)}) async-start(), calls=%async_computation.5 | async-start | bytes 1056768 | tf_op jit(solution)/shard_map/psum | solution.py:11
  168.2 5.3 %copy-start.6 = (f32[32,96,32]{1,2,0:T(8,128)S(1)}, f32[32,96,32]{1,2,0:T(8,128)}, u32[]{:S(2)}) copy-start(f32[32,96,32]{1,2,0:T(8,128)} %reduce_sum.82) | copy-start | bytes 1179652
  168.2 75.6 %copy-start.10 = (f32[128]{0:T(128)S(1)}, f32[128]{0:T(128)}, u32[]{:S(2)}) copy-start(f32[128]{0:T(128)} %param.8) | copy-start | bytes 1540
  173.4 286.1 %all-gather.6.cloned.1.call-start = ((), (), s32[]{:S(2)}) async-start(), calls=%async_computation.6 | async-start | bytes 2359296 | tf_op jit(solution)/shard_map/all_gather | solution.py:19
Sparse Core Ops, SparseCore 0:
  16.3 74.3 all-gather.3
  175.0 281.3 all-reduce.2
Sparse Core Ops, SparseCore 1:
  243.8 61.8 all-gather.5
